TPU v7x, 32 devices: a 4x2x2 block of a 4x4x8 slice. The times are simulated.
32 devices in a mesh: dp: 4 (over y, z), tp: 8 (over x, core).
Axes of the slice: x: 4, y: 2, z: 2, core: 2. Of those that a mesh axis runs over, the one named last changes fastest.
The devices are a block of a 4x4x8 slice.
Arguments:
- X: bfloat16 [8192, 4096], P('dp'), parts along dimension 0
- W: bfloat16 [4096, 32768], P(None, 'tp')
- labels: int32 [8192], P('dp'), parts along dimension 0
Outputs:
- output 1: float32 [4], P('dp'), parts along dimension 0
- output 2: bfloat16 [16384, 32768], P('dp', 'tp'), parts along dimension 0
- output 3: bfloat16 [8192, 4096], P('dp'), parts along dimension 0
There are 4 independent parts. A program takes and returns all parts, laid end to end along the dimension named above; an argument that names none is the same for every part.
All inputs are finite; a program needn't handle non-finite values.
Results may differ from a plain program's by a relative error of at most 0.001.
Values are sent between devices in bfloat16 or wider.
A program may use at most 768 MiB of HBM per device.

v0:
```python
import jax
import jax.numpy as jnp
from jax import lax
from jax.sharding import PartitionSpec as P


def solution(mesh):
    def local(X, W, labels):
        T = X.shape[0]
        Vl = W.shape[1]
        off = lax.axis_index('tp') * Vl
        Z = jnp.dot(X, W, preferred_element_type=jnp.float32)
        m = Z.max(axis=1)
        s = jnp.exp(Z - m[:, None]).sum(axis=1)
        hit = jnp.arange(Vl, dtype=jnp.int32)[None, :] == (labels - off)[:, None]
        z = jnp.where(hit, Z, 0.0).sum(axis=1)
        M = lax.pmax(m, 'tp')
        st = lax.psum(jnp.stack([s * jnp.exp(m - M), z]), 'tp')
        S, zt = st[0], st[1]
        L = jnp.mean(M + jnp.log(S) - zt).reshape(1)
        G = ((jnp.exp(Z - M[:, None]) / S[:, None] - hit.astype(jnp.float32)) / T).astype(jnp.bfloat16)
        dW = jnp.einsum('th,tv->hv', X, G, preferred_element_type=jnp.float32).astype(jnp.bfloat16)
        dXp = jnp.einsum('tv,hv->th', G, W, preferred_element_type=jnp.float32)
        dX = lax.psum(dXp, 'tp').astype(jnp.bfloat16)
        return L, dW, dX

    return jax.shard_map(local, mesh=mesh,
                         in_specs=(P('dp', None), P(None, 'tp'), P('dp')),
                         out_specs=(P('dp'), P('dp', 'tp'), P('dp', None)),
                         check_vma=False)
```

profile of v0, /device:TPU:81, one launch (start us, length us, event | category | flops | bytes accessed | tf_op | source)
XLA Modules:
  0.0 698.4 jit_solution(12661812866087121616)
XLA Ops:
  0.6 1.3 broadcast_subtract_fusion
  1.9 0.0 copy-start
  1.9 78.8 %fusion.1 = (f32[2048]{0:T(1024)S(1)}, f32[2048,4096]{1,0:T(8,128)}) fusion(bf16[2048,4096]{1,0:T(8,128)(2,1)} %param.3, bf16[4096,4096]{1,0:T(8,128)(2,1)} %param.4), kind=kOutput, calls=%fused_computation.10 | convolution fusion | flops 68727865344 | bytes 83894272 | tf_op jit(solution)/shard_map/dot_general | solution.py:12
  80.8 14.1 %pmax.7 = f32[2048]{0:T(1024)S(1)} all-reduce(f32[2048]{0:T(1024)S(1)} %get-tuple-element.10), channel_id=1, replica_groups=mesh['dp'=4,'tp'=8] {'tp'}, use_global_device_ids=true, to_apply=%region_1.0 | all-reduce | flops 2048 | bytes 16384 | tf_op jit(solution)/shard_map/pmax | solution.py:17
  94.8 0.0 copy-done
  94.8 15.2 %exponential_reduce_fusion = (f32[2048]{0:T(1024)S(1)}, f32[2048]{0:T(1024)S(1)}) fusion(f32[2048,4096]{1,0:T(8,128)} %get-tuple-element.11, f32[2048]{0:T(1024)S(1)} %get-tuple-element.10, s32[2048]{0:T(1024)S(1)} %copy-done), kind=kLoop, calls=%fused_computation.4 | loop fusion | flops 41938944 | bytes 33587200 | tf_op jit(solution)/shard_map/reduce_sum | solution.py:14
  110.1 23.0 %psum.14 = f32[2,2048]{1,0:T(2,128)S(1)} all-reduce(f32[2,2048]{1,0:T(2,128)S(1)} %pad_maximum_fusion), channel_id=1, replica_groups=mesh['dp'=4,'tp'=8] {'tp'}, use_global_device_ids=true, to_apply=%region_4.5 | all-reduce | flops 4096 | bytes 32768 | tf_op jit(solution)/shard_map/psum | solution.py:18
  133.1 22.3 %multiply_convert_fusion = bf16[2048,4096]{1,0:T(8,128)(2,1)} fusion(f32[2048,4096]{1,0:T(8,128)} %get-tuple-element.11, f32[2048]{0:T(1024)S(1)} %bitcast.13, f32[2048]{0:T(1024)S(1)} %pmax.7, s32[2048]{0:T(1024)S(1)} %copy-done), kind=kLoop, calls=%fused_computation.1 | loop fusion | flops 58720256 | bytes 50356224 | tf_op jit(solution)/shard_map/convert_element_type | solution.py:21
  155.5 0.6 subtract_reduce_fusion
  156.7 78.6 %fusion.2 = f32[2048,4096]{1,0:T(8,128)} fusion(bf16[2048,4096]{1,0:T(8,128)(2,1)} %multiply_convert_fusion, bf16[4096,4096]{1,0:T(8,128)(2,1)} %param.4), kind=kOutput, calls=%fused_computation.11 | convolution fusion | flops 68719476736 | bytes 83886080 | tf_op jit(solution)/shard_map/tv,hv->th/dot_general | solution.py:23
  235.4 339.1 %all-reduce.1 = bf16[2048,4096]{1,0:T(8,128)(2,1)} all-reduce(f32[2048,4096]{1,0:T(8,128)} %fusion.2), channel_id=1, replica_groups=mesh['dp'=4,'tp'=8] {'tp'}, use_global_device_ids=true, to_apply=%region_6.7 | all-reduce | flops 8388608 | bytes 50331648 | tf_op jit(solution)/shard_map/psum | solution.py:24
  574.5 78.7 %convert_bitcast_fusion = bf16[4096,4096]{0,1:T(8,128)(2,1)} fusion(bf16[2048,4096]{1,0:T(8,128)(2,1)} %multiply_convert_fusion, bf16[2048,4096]{1,0:T(8,128)(2,1)} %param.3), kind=kOutput, calls=%fused_computation | convolution fusion | flops 68736253952 | bytes 67108864 | tf_op jit(solution)/shard_map/th,tv->hv/dot_general | solution.py:22
  653.2 44.1 %copy.6 = bf16[4096,4096]{1,0:T(8,128)(2,1)} copy(bf16[4096,4096]{0,1:T(8,128)(2,1)} %convert_bitcast_fusion) | data formatting | bytes 67108864
  (3 shorter events, 0.0 us)
Async XLA Ops:
  1.9 92.9 %copy-start = (s32[2048]{0:T(1024)S(1)}, s32[2048]{0:T(1024)}, u32[]{:S(2)}) copy-start(s32[2048]{0:T(1024)} %broadcast_subtract_fusion) | copy-start | bytes 24580
where the time goes:
time: 700 us; the launch traced here: 698 us
  blocking collectives  376 us (54%)
  matrix products  236 us (34%)
  local copies, waits for them, and re-layouts  44.1 us (6%)
  other arithmetic  39.5 us (6%)
    psum x1, blocking collectives, local(): dX = lax.psum(dXp, 'tp').astype(jnp.bfloat16)  339 us
    dot_general x1, matrix products, local(): Z = jnp.dot(X, W, preferred_element_type=jnp.float32)  78.8 us
    dot_general x1, matrix products, local(): jnp.einsum('th,tv->hv', X, G, preferred_element_type=jnp.float32)  78.7 us
    dot_general x1, matrix products, local(): dXp = jnp.einsum('tv,hv->th', G, W, preferred_element_type=jnp.float32)  78.6 us
    unnamed x3, local copies, waits for them, and re-layouts  44.1 us
    psum x1, blocking collectives, local(): st = lax.psum(jnp.stack([s * jnp.exp(m - M), z]), 'tp')  23 us
    convert_element_type x1, other arithmetic, local(): ((jnp.exp(Z - M[:, None]) / S[:, None] - hit.astype(jnp.float32)) / T).as...  22.3 us
    reduce_sum x1, other arithmetic, local(): s = jnp.exp(Z - m[:, None]).sum(axis=1)  15.2 us

commit v1 on v0

v1 whole, which is shorter than its diff:
```python
import functools
import math

import jax
import jax.numpy as jnp
from jax import lax
from jax.experimental import pallas as pl
from jax.experimental.pallas import tpu as pltpu
from jax.sharding import PartitionSpec as P

F32 = jnp.float32
BF16 = jnp.bfloat16
MESH = pl.DeviceIdType.MESH

NS = 4
NSL = 8
LANES = 128


def _main(n, nb, T, x_hbm, w_hbm, lab_hbm, g_hbm, dxs_hbm, loss_ref,
          w_v, z_v, x_v, g_v, lab_v, m_s, s_s, t_s, mrep, rrep,
          st_send, st_v, dxb, d2d, r1, r2, s1, s2, fin, o_v,
          w_sem, x_sem, lab_sem, g_sem, st_ssem, st_rsem,
          d2d_ssem, d2d_rsem, s1_ssem, r1_rsem, s2_ssem, r2_rsem, o_sem):
    nch = n // 2
    R = x_v.shape[2]
    BT = n * R
    H, Vl = w_v.shape
    TN = Vl // NS
    TH = H // NS
    inv_t = 1.0 / T
    me = lax.axis_index("tp")
    p, c = me // 2, me % 2
    co = 1 - c
    pr, plf, po = (p + 1) % nch, (p + nch - 1) % nch, (p + 2) % nch
    right, left, partner = {"tp": pr * 2 + c}, {"tp": plf * 2 + c}, {"tp": p * 2 + co}

    def w_copy(j):
        cols = pl.ds(pl.multiple_of(j * TN, TN), TN)
        return pltpu.make_async_copy(w_hbm.at[:, cols], w_v.at[:, cols], w_sem.at[j])

    def rows_of(b):
        return pl.ds(pl.multiple_of(b * R, R), R)

    def x_copy(b):
        return pltpu.make_async_copy(x_hbm.at[:, rows_of(b), :], x_v.at[b % 2], x_sem.at[b % 2])

    def lab_copy(b):
        return pltpu.make_async_copy(lab_hbm.at[:, rows_of(b), :], lab_v.at[b % 3], lab_sem.at[b % 3])

    def g_copy(b):
        return pltpu.make_async_copy(g_v, g_hbm.at[:, rows_of(b), :], g_sem)

    def st_copy(b, d):
        dev = (me + d) % n
        return pltpu.make_async_remote_copy(
            st_send.at[b % 2], st_v.at[b % 2, me], st_ssem.at[b % 2, d], st_rsem.at[b % 2, d],
            device_id={"tp": dev}, device_id_type=MESH)

    def d2d_copy(u):
        return pltpu.make_async_remote_copy(
            dxb.at[u % 2, :, co], d2d.at[u % NSL], d2d_ssem.at[u % 2], d2d_rsem.at[u % NSL],
            device_id=partner, device_id_type=MESH)

    hr = R // 2

    def rs1_copy(u, d):
        return pltpu.make_async_remote_copy(
            s1.at[u % 4, pl.ds(d * hr, hr)], r1.at[u % NSL, d],
            s1_ssem.at[u % 4, d], r1_rsem.at[u % NSL, d],
            device_id=right if d == 0 else left, device_id_type=MESH)

    def rs2_copy(u, d):
        return pltpu.make_async_remote_copy(
            s2.at[u % NSL, d], r2.at[u % NSL, d], s2_ssem.at[u % NSL, d], r2_rsem.at[u % NSL, d],
            device_id=right if d == 0 else left, device_id_type=MESH)

    def o_copy(u):
        b, s = u // NS, u % NS
        return pltpu.make_async_copy(
            o_v.at[u % 2],
            dxs_hbm.at[rows_of(b), pl.ds(pl.multiple_of(s * TH, TH), TH)],
            o_sem.at[u % 2])

    def u1(u):
        d2d_copy(u).wait_recv()
        k, kd = u % 2, u % NSL

        @pl.when(u >= 4)
        def _():
            for d in range(2):
                rs1_copy(u - 4, d).wait_send()

        @pl.when(u >= NSL)
        def _():
            for d in range(2):
                rs2_copy(u - NSL, d).wait_send()
        s1[u % 4] = dxb[k, po, c] + d2d[kd, po]
        for d in range(2):
            rs1_copy(u, d).start()
        s2[kd, 0] = dxb[k, pr, c] + d2d[kd, pr]
        s2[kd, 1] = dxb[k, plf, c] + d2d[kd, plf]
        fin[kd] = dxb[k, p, c] + d2d[kd, p]

    def u2(u):
        kd = u % NSL
        for d in range(2):
            rs1_copy(u, d).wait_recv()
            half = pl.ds(d * hr, hr)
            s2[kd, d, half] = s2[kd, d, half] + r1[kd, d]
            rs2_copy(u, d).start()

    def u3(u):
        kd = u % NSL
        for d in range(2):
            rs2_copy(u, d).wait_recv()

        @pl.when(u >= 2)
        def _():
            o_copy(u - 2).wait()
        o_v[u % 2] = (fin[kd] + r2[kd, 0] + r2[kd, 1]).astype(BF16)
        o_copy(u).start()

    def comm_z(i, j):
        @pl.when(jnp.logical_and(j == 0, i >= 2))
        def _():
            u1((i - 2) * NS + 3)

        @pl.when(jnp.logical_and(j == 0, i >= 3))
        def _():
            u3((i - 3) * NS + 3)

        @pl.when(i >= 2)
        def _():
            u2((i - 2) * NS + j)

    def comm_d(i, s):
        @pl.when(s >= 1)
        def _():
            u1((i - 1) * NS + s - 1)

        @pl.when(jnp.logical_and(s >= 1, i >= 2))
        def _():
            u3((i - 2) * NS + s - 1)

    lane = lax.broadcasted_iota(jnp.int32, (BT, LANES), 1)

    def z_tile(b, j):
        xs = x_v[b % 2].reshape(BT, H)
        lab = lab_v[b % 3].reshape(BT, LANES)
        sub = TN // 2
        for q in range(2):
            base = pl.multiple_of(j * TN + q * sub, sub)
            z = jnp.dot(xs, w_v[:, pl.ds(base, sub)], preferred_element_type=F32)
            z_v[b % 2, :, pl.ds(base, sub)] = z
            zs = [z[:, k * LANES:(k + 1) * LANES] for k in range(sub // LANES)]
            m_old = m_s[...]
            m_new = functools.reduce(jnp.maximum, zs, m_old)
            acc = s_s[...] * jnp.exp(m_old - m_new)
            tgt = t_s[...]
            for k, zk in enumerate(zs):
                acc = acc + jnp.exp(zk - m_new)
                tgt = tgt + jnp.where(lab == lane + (base + k * LANES), zk, 0.0)
            m_s[...] = m_new
            s_s[...] = acc
            t_s[...] = tgt

    def g_tile(b, j):
        lab = lab_v[b % 3].reshape(BT, LANES)
        for k in range(TN // LANES):
            base = pl.multiple_of(j * TN + k * LANES, LANES)
            z = z_v[b % 2, :, pl.ds(base, LANES)]
            pr_ = jnp.exp(z - mrep[...]) * rrep[...]
            hit = jnp.where(lab == lane + base, 1.0, 0.0)
            g = ((pr_ - hit) * inv_t).astype(BF16)
            g_v[:, :, pl.ds(base, LANES)] = g.reshape(n, R, LANES)

    def stats_init():
        m_s[...] = jnp.full((BT, LANES), -jnp.inf, F32)
        s_s[...] = jnp.zeros((BT, LANES), F32)
        t_s[...] = jnp.zeros((BT, LANES), F32)

    def stats_send(b):
        ml = m_s[...]
        m = jnp.max(ml, axis=1, keepdims=True)
        s = jnp.sum(s_s[...] * jnp.exp(ml - m), axis=1, keepdims=True)
        t = jnp.sum(t_s[...], axis=1, keepdims=True)
        a = jnp.where(lane == 0, m, jnp.where(lane == 1, s, t))
        a = a.T[0:8]
        st_send[b % 2] = a
        st_v[b % 2, me] = a
        for d in range(1, n):
            st_copy(b, d).start()

    def stats_recv(b):
        k = b % 2
        for d in range(1, n):
            st_copy(b, d).wait()
        ms = st_v[k, :, 0, :]
        m = jnp.max(ms, axis=0, keepdims=True)
        s = jnp.sum(st_v[k, :, 1, :] * jnp.exp(ms - m), axis=0, keepdims=True)
        t = jnp.sum(st_v[k, :, 2, :], axis=0, keepdims=True)
        loss_ref[...] += m + jnp.log(s) - t
        row = lax.broadcasted_iota(jnp.int32, (LANES, BT), 0)
        a = jnp.where(row == 0, m, 1.0 / s).T
        mrep[...] = jnp.broadcast_to(a[:, 0:1], (BT, LANES))
        rrep[...] = jnp.broadcast_to(a[:, 1:2], (BT, LANES))

    def d_tile(b, s):
        u = b * NS + s

        @pl.when(u >= 2)
        def _():
            d2d_copy(u - 2).wait_send()
        gs = g_v[...].reshape(BT, H if False else Vl)
        dx = lax.dot_general(gs, w_v[pl.ds(pl.multiple_of(s * TH, TH), TH), :],
                             (((1,), (1,)), ((), ())), preferred_element_type=F32)
        dxb[u % 2] = dx.reshape(nch, 2, R, TH)
        d2d_copy(u).start()

    for j in range(NS):
        w_copy(j).start()
        if j == 0:
            x_copy(0).start()
            lab_copy(0).start()
            lab_copy(1).start()
            x_copy(1).start()
    bar = pltpu.get_barrier_semaphore()
    for d in range(1, n):
        pl.semaphore_signal(bar, inc=1, device_id={"tp": (me + d) % n}, device_id_type=MESH)
    pl.semaphore_wait(bar, n - 1)

    loss_ref[...] = jnp.zeros_like(loss_ref)
    stats_init()
    x_copy(0).wait()
    lab_copy(0).wait()

    @pl.loop(0, NS)
    def _(j):
        w_copy(j).wait()
        z_tile(0, j)
    stats_send(0)

    @pl.loop(1, nb)
    def _(i):
        x_copy(i).wait()
        lab_copy(i).wait()
        stats_recv(i - 1)
        stats_init()

        @pl.when(i >= 2)
        def _():
            g_copy(i - 2).wait()

        @pl.when(i + 1 < nb)
        def _():
            x_copy(i + 1).start()
            lab_copy(i + 1).start()

        @pl.loop(0, NS)
        def _(j):
            comm_z(i, j)
            z_tile(i, j)
            g_tile(i - 1, j)
        stats_send(i)
        g_copy(i - 1).start()

        @pl.loop(0, NS)
        def _(s):
            comm_d(i, s)
            d_tile(i - 1, s)

    stats_recv(nb - 1)
    g_copy(nb - 2).wait()

    @pl.loop(0, NS)
    def _(j):
        comm_z(nb, j)
        g_tile(nb - 1, j)
    g_copy(nb - 1).start()

    @pl.loop(0, NS)
    def _(s):
        comm_d(nb, s)
        d_tile(nb - 1, s)

    nu = nb * NS

    @pl.loop(0, NS)
    def _(j):
        comm_z(nb + 1, j)

    @pl.loop(0, NS)
    def _(j):
        u3((nb - 1) * NS + j)

    for u in range(nu - 2, nu):
        d2d_copy(u).wait_send()
        o_copy(u).wait()
    for u in range(nu - 4, nu):
        for d in range(2):
            rs1_copy(u, d).wait_send()
    for u in range(nu - NSL, nu):
        for d in range(2):
            rs2_copy(u, d).wait_send()
    g_copy(nb - 1).wait()


def _dw(x_ref, g_ref, o_ref):
    o_ref[...] = lax.dot_general(x_ref[...], g_ref[...], (((0,), (0,)), ((), ())),
                                 preferred_element_type=F32).astype(BF16)


def solution(mesh):
    n = mesh.shape["tp"]

    def local(X, W, labels):
        T, H = X.shape
        Vl = W.shape[1]
        own = T // n
        R = 32
        nb = own // R
        BT = n * R
        TH = H // NS
        off = lax.axis_index("tp") * Vl
        lab = jnp.broadcast_to((labels - off)[:, None], (T, LANES)).reshape(n, own, LANES)
        hbm = pl.BlockSpec(memory_space=pl.ANY)
        vm = pltpu.VMEM
        dma = pltpu.SemaphoreType.DMA
        flops = 4 * T * H * Vl
        g, dxs, loss = pl.pallas_call(
            functools.partial(_main, n, nb, T),
            out_shape=(jax.ShapeDtypeStruct((n, own, Vl), BF16),
                       jax.ShapeDtypeStruct((own, H), BF16),
                       jax.ShapeDtypeStruct((1, BT), F32)),
            in_specs=[hbm, hbm, hbm],
            out_specs=(hbm, hbm, pl.BlockSpec(memory_space=pltpu.VMEM)),
            scratch_shapes=[
                vm((H, Vl), BF16), vm((2, BT, Vl), F32), vm((2, n, R, H), BF16),
                vm((n, R, Vl), BF16), vm((3, n, R, LANES), jnp.int32),
                vm((BT, LANES), F32), vm((BT, LANES), F32), vm((BT, LANES), F32),
                vm((BT, LANES), F32), vm((BT, LANES), F32),
                vm((2, 8, BT), F32), vm((2, n, 8, BT), F32),
                vm((2, n // 2, 2, R, TH), F32), vm((NSL, n // 2, R, TH), F32),
                vm((NSL, 2, R // 2, TH), F32), vm((NSL, 2, R, TH), F32),
                vm((4, R, TH), F32), vm((NSL, 2, R, TH), F32), vm((NSL, R, TH), F32),
                vm((2, R, TH), BF16),
                dma((NS,)), dma((2,)), dma((3,)), dma, dma((2, n)), dma((2, n)),
                dma((2,)), dma((NSL,)), dma((4, 2)), dma((NSL, 2)), dma((NSL, 2)),
                dma((NSL, 2)), dma((2,)),
            ],
            compiler_params=pltpu.CompilerParams(
                collective_id=0, has_side_effects=True, vmem_limit_bytes=67043328),
            cost_estimate=pl.CostEstimate(flops=flops, bytes_accessed=2 * (H * Vl + T * (H + Vl)),
                                          transcendentals=2 * T * Vl),
            name="head_main",
        )(X.reshape(n, own, H), W, lab)
        G = g.reshape(T, Vl)
        dX = lax.all_gather(dxs, "tp", axis=0, tiled=True)
        th, tv = 1024, 1024
        dW = pl.pallas_call(
            _dw,
            out_shape=jax.ShapeDtypeStruct((H, Vl), BF16),
            grid=(Vl // tv, H // th),
            in_specs=[pl.BlockSpec((T, th), lambda v, h: (0, h)),
                      pl.BlockSpec((T, tv), lambda v, h: (0, v))],
            out_specs=pl.BlockSpec((th, tv), lambda v, h: (h, v)),
            compiler_params=pltpu.CompilerParams(vmem_limit_bytes=48 * 1024 * 1024),
            cost_estimate=pl.CostEstimate(flops=2 * T * H * Vl,
                                          bytes_accessed=2 * (H * Vl + T * (H + Vl)),
                                          transcendentals=0),
            name="head_dw",
        )(X, G)
        L = (jnp.sum(loss) / T).reshape(1)
        return L, dW, dX

    return jax.shard_map(local, mesh=mesh,
                         in_specs=(P('dp', None), P(None, 'tp'), P('dp')),
                         out_specs=(P('dp'), P('dp', 'tp'), P('dp', None)),
                         check_vma=False)
```

time: 700 us -> 382 us (0.55)
  blocking collectives: 376 us -> 0 us
  Pallas kernels: 0 us -> 343 us
  matrix products: 236 us -> 0 us
  other arithmetic: 39.5 us -> 1.94 us
  local copies, waits for them, and re-layouts: 44.1 us -> 15.4 us
  between operations: 2.46 us -> 15.8 us
    psum x2 -> x0, blocking collectives: 362 us -> none  [the longest x1 339 us: local(): dX = lax.psum(dXp, 'tp').astype(jnp.bfloat16)]
    pallas_call x0 -> x2, Pallas kernels: none -> 343 us  [the longest x1 265 us: local(): pl.pallas_call(functools.partial(_main, n, nb, T), out_shape=(jax.ShapeDt...]
    dot_general x3 -> x0, matrix products: 236 us -> none  [the longest x1 78.8 us: local(): Z = jnp.dot(X, W, preferred_element_type=jnp.float32)]
    unnamed x3 -> x1, local copies, waits for them, and re-layouts: 44.1 us -> 14.1 us
    convert_element_type x1 -> x0, other arithmetic: 22.3 us -> none  [local(): ((jnp.exp(Z - M[:, None]) / S[:, None] - hit.astype(jnp.float32)) / T).as...]
    reduce_sum x2 -> x1, other arithmetic: 15.8 us -> 1.24 us  [local(): L = (jnp.sum(loss) / T).reshape(1)]
    pmax x1 -> x0, blocking collectives: 14.1 us -> none  [local(): M = lax.pmax(m, 'tp')]
  transfers between devices with their start and end apart: 0 -> 1, of which waited for: 0 -> 1; matrix products, arithmetic and copies ran while one was open for 0% -> 0% of each run, Pallas kernels for 0% -> 20%
where the time goes in v1:
time: 382 us
  Pallas kernels  343 us (90%)
  between operations  15.8 us (4%)
  local copies, waits for them, and re-layouts  15.4 us (4%)
  waiting for transfers between devices  5.96 us (2%)
    pallas_call x1, Pallas kernels, local(): pl.pallas_call(functools.partial(_main, n, nb, T), out_shape=(jax.ShapeDt...  265 us
    pallas_call x1, Pallas kernels, local(): pl.pallas_call(_dw, out_shape=jax.ShapeDtypeStruct((H, Vl), BF16), grid=(...  77.8 us
    unnamed x1, local copies, waits for them, and re-layouts  14.1 us
  transfers between devices with their start and end apart: 1, of which 1 were waited for; matrix products, arithmetic and copies ran while one was open for 0% of the time, Pallas kernels for 20%

profile of v1, /device:TPU:81, one launch (start us, length us, event | category | flops | bytes accessed | tf_op | source)
XLA Modules:
  0.0 382.1 jit_solution(12391782322346414838)
XLA Ops:
  7.2 0.1 all-gather.2.cloned.1.call-start
  7.2 0.7 broadcast_subtract_fusion
  8.0 1.3 broadcast_in_dim.9.lab_hbm
  9.3 265.1 %head_main.1 = (bf16[8,256,4096]{2,1,0:T(8,128)(2,1)}, bf16[256,4096]{1,0:T(8,128)(2,1)}, f32[1,256]{1,0:T(1,128)}) custom-call(bf16[8,256,4096]{2,1,0:T(8,128)(2,1)} %bitcast.3, bf16[4096,4096]{1,0:T(8,128)(2,1)} %w_hbm.1, s32[8,256,128]{2,1,0:T(8,128)} %broadcast_in_dim.9.lab_hbm), custom_call_target="tpu_custom_call" | custom-call | flops 137438953472 | bytes 67108864 | tf_op jit(solution)/shard_map/head_main/pallas_call | solution.py:331
  274.3 0.1 all-gather.2.cloned.1.call-update
  274.4 1.2 reduce_sum.9
  276.3 77.8 %head_dw.1 = bf16[4096,4096]{1,0:T(8,128)(2,1)} custom-call(bf16[2048,4096]{1,0:T(8,128)(2,1)} %x_ref.1, bf16[2048,4096]{1,0:T(8,128)(2,1)} %bitcast.4), custom_call_target="tpu_custom_call" | custom-call | flops 68719476736 | bytes 67108864 | tf_op jit(solution)/shard_map/head_dw/pallas_call | solution.py:361
  354.1 5.9 %all-gather.2.cloned.1.call-done = bf16[2048,4096]{1,0:T(8,128)(2,1)} async-done(((bf16[256,4096]{1,0:T(8,128)(2,1)}), bf16[2048,4096]{1,0:T(8,128)(2,1)}) %all-gather.2.cloned.1.call-update) | async-done | bytes 16777232 | tf_op jit(solution)/shard_map/all_gather | solution.py:359
  360.0 14.1 %copy.7 = bf16[2048,4096]{1,0:T(8,128)(2,1)} copy(bf16[2048,4096]{1,0:T(8,128)(2,1)} %all-gather.2.cloned.1.call-done) | data formatting | bytes 33554432
  (1 shorter events, 0.0 us)
Async XLA Ops:
  7.2 352.9 %all-gather.2.cloned.1.call-start = ((), (), s32[]{:S(2)}) async-start(), calls=%async_computation | async-start | bytes 18874368 | tf_op jit(solution)/shard_map/all_gather | solution.py:359
Sparse Core Ops, SparseCore 0:
  274.5 85.4 all-gather.1

commit v2 on v0

v2 whole, which is shorter than its diff:
```python
import functools
import math

import jax
import jax.numpy as jnp
from jax import lax
from jax.experimental import pallas as pl
from jax.experimental.pallas import tpu as pltpu
from jax.sharding import PartitionSpec as P

F32 = jnp.float32
BF16 = jnp.bfloat16
MESH = pl.DeviceIdType.MESH

NS = 4
NSL = 8
LANES = 128
TD = 512
NT = 6


def _main(n, nb, T, x_hbm, w_hbm, lab_hbm, g_hbm, dxf_hbm, dw1_hbm, loss_ref,
          lab_v, m_s, s_s, t_s, mrep, rrep,
          st_send, st_v, dxb, d2d, r1, r2, s1, s2, fin, o_v,
          w_sem, x_sem, lab_sem, g_sem, st_ssem, st_rsem,
          d2d_ssem, d2d_rsem, s1_ssem, r1_rsem, s2_ssem, r2_rsem, o_sem,
          ag_ssem, ag_rsem, xt_sem, gt_sem, ot_sem):
    nch = n // 2
    own = x_hbm.shape[1]
    R = lab_v.shape[2]
    BT = n * R
    H, Vl = w_hbm.shape
    TN = Vl // NS
    TH = H // NS
    inv_t = 1.0 / T
    me = lax.axis_index("tp")
    p, c = me // 2, me % 2
    co = 1 - c
    pr, plf, po = (p + 1) % nch, (p + nch - 1) % nch, (p + 2) % nch
    right, left, partner = {"tp": pr * 2 + c}, {"tp": plf * 2 + c}, {"tp": p * 2 + co}

    def rows_of(b):
        return pl.ds(pl.multiple_of(b * R, R), R)

    def lab_copy(b):
        return pltpu.make_async_copy(lab_hbm.at[:, rows_of(b), :], lab_v.at[b % 3], lab_sem.at[b % 3])

    def st_copy(b, d):
        dev = (me + d) % n
        return pltpu.make_async_remote_copy(
            st_send.at[b % 2], st_v.at[b % 2, me], st_ssem.at[b % 2, d], st_rsem.at[b % 2, d],
            device_id={"tp": dev}, device_id_type=MESH)

    def d2d_copy(u):
        return pltpu.make_async_remote_copy(
            dxb.at[u % 3, :, co], d2d.at[u % NSL], d2d_ssem.at[u % 3], d2d_rsem.at[u % NSL],
            device_id=partner, device_id_type=MESH)

    hr = R // 2

    def rs1_copy(u, d):
        return pltpu.make_async_remote_copy(
            s1.at[u % 4, pl.ds(d * hr, hr)], r1.at[u % NSL, d],
            s1_ssem.at[u % 4, d], r1_rsem.at[u % NSL, d],
            device_id=right if d == 0 else left, device_id_type=MESH)

    def rs2_copy(u, d):
        return pltpu.make_async_remote_copy(
            s2.at[u % NSL, d], r2.at[u % NSL, d], s2_ssem.at[u % NSL, d], r2_rsem.at[u % NSL, d],
            device_id=right if d == 0 else left, device_id_type=MESH)

    def o_copy(u):
        b, s = u // NS, u % NS
        return pltpu.make_async_copy(
            o_v.at[s], dxf_hbm.at[me, rows_of(b), pl.ds(pl.multiple_of(s * TH, TH), TH)],
            o_sem.at[s])

    opp = po * 2 + c
    qr, ql = pr * 2 + c, plf * 2 + c

    def ag_copy(kind, k, owner, lo, rows, dev):
        r = pl.ds(pl.multiple_of(k * R + lo, rows), rows)
        return pltpu.make_async_remote_copy(
            dxf_hbm.at[owner, r], dxf_hbm.at[owner, r], ag_ssem.at[kind, k], ag_rsem.at[kind, k],
            device_id=dev, device_id_type=MESH)

    def ag_all(k):
        args = [(me, 0, R, right), (me, 0, R, left), (me, 0, R, partner),
                (ql, 0, hr, right), (qr, hr, hr, left),
                (ql, 0, R, partner), (qr, 0, R, partner), (opp, 0, R, partner)]
        return [functools.partial(ag_copy, i, k, *x) for i, x in enumerate(args)]

    def ag_a(k):
        cs = ag_all(k)
        for i in (0, 1, 2):
            cs[i]().start()

    def ag_b(k):
        cs = ag_all(k)
        for i in (0, 1):
            cs[i]().wait_recv()
        for i in (3, 4, 5, 6):
            cs[i]().start()

    def ag_c(k):
        cs = ag_all(k)
        for i in (3, 4):
            cs[i]().wait_recv()
        cs[7]().start()

    def ag_end(k):
        cs = ag_all(k)
        for i in (2, 5, 6, 7):
            cs[i]().wait_recv()
        for cp in cs:
            cp().wait_send()

    def u1(u):
        d2d_copy(u).wait_recv()
        k, kd = u % 3, u % NSL

        @pl.when(u >= 4)
        def _():
            for d in range(2):
                rs1_copy(u - 4, d).wait_send()

        @pl.when(u >= NSL)
        def _():
            for d in range(2):
                rs2_copy(u - NSL, d).wait_send()
        s1[u % 4] = dxb[k, po, c] + d2d[kd, po]
        for d in range(2):
            rs1_copy(u, d).start()
        s2[kd, 0] = dxb[k, pr, c] + d2d[kd, pr]
        s2[kd, 1] = dxb[k, plf, c] + d2d[kd, plf]
        fin[kd] = dxb[k, p, c] + d2d[kd, p]

    def u2(u):
        kd = u % NSL
        for d in range(2):
            rs1_copy(u, d).wait_recv()
            half = pl.ds(d * hr, hr)
            s2[kd, d, half] = s2[kd, d, half] + r1[kd, d]
            rs2_copy(u, d).start()

    def u3(u):
        kd = u % NSL
        for d in range(2):
            rs2_copy(u, d).wait_recv()
        o_v[u % NS] = (fin[kd] + r2[kd, 0] + r2[kd, 1]).astype(BF16)
        o_copy(u).start()

    def when(cond):
        return pl.when(cond)

    def o_wait(b):
        for s in range(NS):
            o_copy(b * NS + s).wait()

    def comm_z(i, j):
        @when(jnp.logical_and(j < 2, i >= 2))
        def _():
            u1((i - 2) * NS + 2 + j)

        @when(jnp.logical_and(j < 3, i >= 3))
        def _():
            u3((i - 3) * NS + 1 + j)

        @when(jnp.logical_and(j >= 2, i >= 2))
        def _():
            u2((i - 2) * NS + j - 2)

    def comm_d(i, s):
        @when(jnp.logical_and(s < 2, i >= 2))
        def _():
            u2((i - 2) * NS + 2 + s)

        @when(s >= 2)
        def _():
            u1((i - 1) * NS + s - 2)

        @when(jnp.logical_and(s == 3, i >= 2))
        def _():
            u3((i - 2) * NS)

        @when(jnp.logical_and(s == 2, i >= 3))
        def _():
            o_wait(i - 3)

        @when(jnp.logical_and(s == 2, jnp.logical_and(i >= 5, i % 2 == 1)))
        def _():
            ag_c((i - 5) // 2)

        @when(jnp.logical_and(s == 2, jnp.logical_and(i >= 3, i % 2 == 1)))
        def _():
            ag_a((i - 3) // 2)

        @when(jnp.logical_and(s == 2, jnp.logical_and(i >= 4, i % 2 == 0)))
        def _():
            ag_b((i - 4) // 2)

    lane = lax.broadcasted_iota(jnp.int32, (BT, LANES), 1)

    bar = pltpu.get_barrier_semaphore()
    for d in range(1, n):
        pl.semaphore_signal(bar, inc=1, device_id={"tp": (me + d) % n}, device_id_type=MESH)
    pl.semaphore_wait(bar, n - 1)

    def phase1(w_v, z_v, x_v, g_v):
        def w_copy(j):
            cols = pl.ds(pl.multiple_of(j * TN, TN), TN)
            return pltpu.make_async_copy(w_hbm.at[:, cols], w_v.at[:, cols], w_sem.at[j])

        def x_copy(b):
            return pltpu.make_async_copy(x_hbm.at[:, rows_of(b), :], x_v.at[b % 2], x_sem.at[b % 2])

        def g_copy(b):
            return pltpu.make_async_copy(g_v, g_hbm.at[:, rows_of(b), :], g_sem)

        def z_tile(b, j):
            cols = pl.ds(pl.multiple_of(j * TN, TN), TN)
            z_v[:, cols] = jnp.dot(x_v[b % 2].reshape(BT, H), w_v[:, cols],
                                          preferred_element_type=F32)

        def stat_tile(b, j):
            for r in range(0, BT, 16):
                rows = pl.ds(r, 16)
                lab = lab_v[b % 3].reshape(BT, LANES)[r:r + 16]
                ln = lane[r:r + 16]
                zs = [z_v[rows, pl.ds(pl.multiple_of(j * TN + k * LANES, LANES), LANES)]
                      for k in range(TN // LANES)]
                m_old = m_s[rows]
                m_new = functools.reduce(jnp.maximum, zs, m_old)
                acc = s_s[rows] * jnp.exp(m_old - m_new)
                tgt = t_s[rows]
                for k, zk in enumerate(zs):
                    acc = acc + jnp.exp(zk - m_new)
                    tgt = tgt + jnp.where(lab == ln + (j * TN + k * LANES), zk, 0.0)
                m_s[rows] = m_new
                s_s[rows] = acc
                t_s[rows] = tgt

        def g_tile(b, j):
            rb = 2 * R
            for r in range(0, BT, rb):
                rows = pl.ds(r, rb)
                lab = lab_v[b % 3].reshape(BT, LANES)[r:r + rb]
                ln = lane[r:r + rb]
                mm, rr = mrep[rows], rrep[rows]
                for k in range(TN // LANES):
                    base = pl.multiple_of(j * TN + k * LANES, LANES)
                    z = z_v[rows, pl.ds(base, LANES)]
                    e = jnp.exp(z - mm) * rr
                    g = (e - jnp.where(lab == ln + base, 1.0, 0.0)) * inv_t
                    g_v[pl.ds(r // R, rb // R), :, pl.ds(base, LANES)] = (
                        g.astype(BF16).reshape(rb // R, R, LANES))

        def stats_init():
            m_s[...] = jnp.full((BT, LANES), -jnp.inf, F32)
            s_s[...] = jnp.zeros((BT, LANES), F32)
            t_s[...] = jnp.zeros((BT, LANES), F32)

        def stats_send(b):
            ml = m_s[...]
            m = jnp.max(ml, axis=1, keepdims=True)
            s = jnp.sum(s_s[...] * jnp.exp(ml - m), axis=1, keepdims=True)
            t = jnp.sum(t_s[...], axis=1, keepdims=True)
            a = jnp.where(lane == 0, m, jnp.where(lane == 1, s, t))
            a = a.T[0:8]
            st_send[b % 2] = a
            st_v[b % 2, me] = a
            for d in range(1, n):
                st_copy(b, d).start()

        def stats_recv(b):
            k = b % 2
            for d in range(1, n):
                st_copy(b, d).wait()
            ms = st_v[k, :, 0, :]
            m = jnp.max(ms, axis=0, keepdims=True)
            s = jnp.sum(st_v[k, :, 1, :] * jnp.exp(ms - m), axis=0, keepdims=True)
            t = jnp.sum(st_v[k, :, 2, :], axis=0, keepdims=True)
            loss_ref[...] += m + jnp.log(s) - t
            row = lax.broadcasted_iota(jnp.int32, (LANES, BT), 0)
            a = jnp.where(row == 0, m, 1.0 / s).T
            mrep[...] = jnp.broadcast_to(a[:, 0:1], (BT, LANES))
            rrep[...] = jnp.broadcast_to(a[:, 1:2], (BT, LANES))

        def d_tile(b, s):
            u = b * NS + s

            @pl.when(u >= 3)
            def _():
                d2d_copy(u - 3).wait_send()
            gs = g_v[...].reshape(BT, Vl)
            dx = lax.dot_general(gs, w_v[pl.ds(pl.multiple_of(s * TH, TH), TH), :],
                                 (((1,), (1,)), ((), ())), preferred_element_type=F32)
            dxb[u % 3] = dx.reshape(nch, 2, R, TH)
            d2d_copy(u).start()

        for j in range(NS):
            w_copy(j).start()
            if j == 0:
                x_copy(0).start()
                lab_copy(0).start()
                lab_copy(1).start()
                x_copy(1).start()
        loss_ref[...] = jnp.zeros_like(loss_ref)
        stats_init()
        x_copy(0).wait()
        lab_copy(0).wait()

        @pl.loop(0, NS)
        def _(j):
            w_copy(j).wait()
            z_tile(0, j)

        @pl.loop(0, NS)
        def _(j):
            stat_tile(0, j)
        stats_send(0)

        @pl.loop(1, nb)
        def _(i):
            x_copy(i).wait()
            lab_copy(i).wait()
            stats_recv(i - 1)
            stats_init()

            @pl.when(i >= 2)
            def _():
                g_copy(i - 2).wait()

            @pl.when(i + 1 < nb)
            def _():
                x_copy(i + 1).start()
                lab_copy(i + 1).start()

            @pl.loop(0, NS)
            def _(j):
                comm_z(i, j)

                @pl.when(j > 0)
                def _():
                    stat_tile(i, j - 1)
                g_tile(i - 1, j)
                z_tile(i, j)
            stat_tile(i, NS - 1)
            stats_send(i)
            g_copy(i - 1).start()

            @pl.loop(0, NS)
            def _(s):
                comm_d(i, s)
                d_tile(i - 1, s)

        stats_recv(nb - 1)
        g_copy(nb - 2).wait()

        @pl.loop(0, NS)
        def _(j):
            comm_z(nb, j)
            g_tile(nb - 1, j)
        g_copy(nb - 1).start()

        @pl.loop(0, NS)
        def _(s):
            comm_d(nb, s)
            d_tile(nb - 1, s)

        g_copy(nb - 1).wait()

    nu = nb * NS

    def phase2(xt, gt, ot):
        th = xt.shape[3]
        nv = NS
        tv = Vl // nv
        nt = dw1_hbm.shape[0] // th

        def xt_copy(h):
            cols = pl.ds(pl.multiple_of(h * th, th), th)
            return pltpu.make_async_copy(x_hbm.at[:, :, cols], xt.at[h % 2], xt_sem.at[h % 2])

        def gt_copy(v):
            cols = pl.ds(pl.multiple_of(v * tv, tv), tv)
            return pltpu.make_async_copy(g_hbm.at[:, :, cols], gt.at[:, :, cols], gt_sem.at[v])

        def ot_copy(t):
            h, v = t // nv, t % nv
            return pltpu.make_async_copy(
                ot.at[t % 2],
                dw1_hbm.at[pl.ds(pl.multiple_of(h * th, th), th), pl.ds(pl.multiple_of(v * tv, tv), tv)],
                ot_sem.at[t % 2])

        xt_copy(0).start()
        for v in range(nv):
            gt_copy(v).start()

        @pl.loop(0, nt * nv)
        def _(t):
            h, v = t // nv, t % nv

            @pl.when(t < NS)
            def _():
                comm_z(nb + 1, t)

            @pl.when(jnp.logical_and(t >= 4, t < 6))
            def _():
                u2(nu - 2 + t - 4)

            @pl.when(jnp.logical_and(t >= 7, t < 7 + NS))
            def _():
                u3(nu - NS + t - 7)

            for when_, (step_, k0) in ((1, (ag_a, 3)), (6, (o_wait, 6)), (6, (ag_c, 2)), (6, (ag_b, 3)),
                                       (6, (ag_a, 4)), (6, (ag_a, 5)), (9, (ag_a, 6)),
                                       (12, (o_wait, 7)), (12, (ag_a, 7)), (13, (ag_c, 3)),
                                       (14, (ag_b, 4)), (17, (ag_b, 5)), (19, (ag_b, 6)),
                                       (22, (ag_c, 4)), (22, (ag_b, 7)), (23, (ag_c, 5))):
                @pl.when(t == when_)
                def _(step_=step_, k0=k0):
                    step_(k0)

            @pl.when(v == 0)
            def _():
                xt_copy(h).wait()

            @pl.when(jnp.logical_and(v == 0, h + 1 < nt))
            def _():
                xt_copy(h + 1).start()

            @pl.when(h == 0)
            def _():
                gt_copy(v).wait()

            @pl.when(t >= 2)
            def _():
                ot_copy(t - 2).wait()
            cols = pl.ds(pl.multiple_of(v * tv, tv), tv)
            ot[t % 2] = lax.dot_general(
                xt[h % 2].reshape(T, th), gt[:, :, cols].reshape(T, tv),
                (((0,), (0,)), ((), ())), preferred_element_type=F32).astype(BF16)
            ot_copy(t).start()

        for t in range(nt * nv - 2, nt * nv):
            ot_copy(t).wait()

    vm = pltpu.VMEM
    pl.run_scoped(phase1, vm((H, Vl), BF16), vm((BT, Vl), F32), vm((2, n, R, H), BF16),
                  vm((n, R, Vl), BF16))
    th = TD
    pl.run_scoped(phase2, vm((2, n, own, th), BF16), vm((n, own, Vl), BF16),
                  vm((2, th, Vl // NS), BF16))

    ag_c(6)
    ag_c(7)
    for k in range(nb):
        ag_end(k)
    for u in range(nu - 3, nu):
        d2d_copy(u).wait_send()
    for u in range(nu - 4, nu):
        for d in range(2):
            rs1_copy(u, d).wait_send()
    for u in range(nu - NSL, nu):
        for d in range(2):
            rs2_copy(u, d).wait_send()


def _rest(inv_t, x_hbm, g_hbm, dw1_hbm, dxf_hbm, loss_ref, dw_hbm, dx_hbm, l_ref,
          xt, gt, ot, cb, xt_sem, gt_sem, ot_sem, rd_sem, wr_sem):
    T, H = x_hbm.shape
    Vl = g_hbm.shape[1]
    nv, th = NS, TD
    tv = Vl // nv
    nh = H // th - NT
    rows, nbuf = cb.shape[1], cb.shape[0]
    ahead = nbuf // 2
    ndx = T // rows
    nc = ndx + NT * th // rows
    per = -(-nc // (nh * nv))

    def xt_copy(h):
        cols = pl.ds(pl.multiple_of((h + NT) * th, th), th)
        return pltpu.make_async_copy(x_hbm.at[:, cols], xt.at[h % 2], xt_sem.at[h % 2])

    def gt_copy(v):
        cols = pl.ds(pl.multiple_of(v * tv, tv), tv)
        return pltpu.make_async_copy(g_hbm.at[:, cols], gt.at[:, cols], gt_sem.at[v])

    def ot_copy(t):
        h, v = t // nv, t % nv
        return pltpu.make_async_copy(
            ot.at[t % 2],
            dw_hbm.at[pl.ds(pl.multiple_of((h + NT) * th, th), th), pl.ds(pl.multiple_of(v * tv, tv), tv)],
            ot_sem.at[t % 2])

    def rd_start(c):
        @pl.when(c < ndx)
        def _():
            r = pl.ds(pl.multiple_of(c * rows, rows), rows)
            pltpu.make_async_copy(dxf_hbm.at[r], cb.at[c % nbuf], rd_sem.at[c % nbuf]).start()

        @pl.when(jnp.logical_and(c >= ndx, c < nc))
        def _():
            r = pl.ds(pl.multiple_of((c - ndx) * rows, rows), rows)
            pltpu.make_async_copy(dw1_hbm.at[r], cb.at[c % nbuf], rd_sem.at[c % nbuf]).start()

    def rd_wait(c):
        pltpu.make_async_copy(dxf_hbm.at[pl.ds(0, rows)], cb.at[c % nbuf], rd_sem.at[c % nbuf]).wait()

    def wr_start(c):
        @pl.when(c < ndx)
        def _():
            r = pl.ds(pl.multiple_of(c * rows, rows), rows)
            pltpu.make_async_copy(cb.at[c % nbuf], dx_hbm.at[r], wr_sem.at[c % nbuf]).start()

        @pl.when(c >= ndx)
        def _():
            r = pl.ds(pl.multiple_of((c - ndx) * rows, rows), rows)
            pltpu.make_async_copy(cb.at[c % nbuf], dw_hbm.at[r], wr_sem.at[c % nbuf]).start()

    def wr_wait(c):
        pltpu.make_async_copy(cb.at[c % nbuf], dx_hbm.at[pl.ds(0, rows)], wr_sem.at[c % nbuf]).wait()

    xt_copy(0).start()
    for v in range(nv):
        gt_copy(v).start()
    for c in range(ahead):
        rd_start(c)
    l_ref[0] = jnp.sum(loss_ref[...]) * inv_t

    @pl.loop(0, nh * nv)
    def _(t):
        h, v = t // nv, t % nv

        @pl.loop(0, per)
        def _(q):
            c = t * per + q

            @pl.when(c < nc)
            def _():
                rd_wait(c)
                wr_start(c)

                @pl.when(c >= ahead)
                def _():
                    wr_wait(c - ahead)
                rd_start(c + ahead)

        @pl.when(v == 0)
        def _():
            xt_copy(h).wait()

        @pl.when(jnp.logical_and(v == 0, h + 1 < nh))
        def _():
            xt_copy(h + 1).start()

        @pl.when(h == 0)
        def _():
            gt_copy(v).wait()

        @pl.when(t >= 2)
        def _():
            ot_copy(t - 2).wait()
        cols = pl.ds(pl.multiple_of(v * tv, tv), tv)
        ot[t % 2] = lax.dot_general(xt[h % 2], gt[:, cols], (((0,), (0,)), ((), ())),
                                    preferred_element_type=F32).astype(BF16)
        ot_copy(t).start()

    for t in range(nh * nv - 2, nh * nv):
        ot_copy(t).wait()
    for c in range(nc - ahead, nc):
        wr_wait(c)


def solution(mesh):
    n = mesh.shape["tp"]

    def local(X, W, labels):
        T, H = X.shape
        Vl = W.shape[1]
        own = T // n
        R = 32
        nb = own // R
        BT = n * R
        TH = H // NS
        off = lax.axis_index("tp") * Vl
        lab = jnp.broadcast_to((labels - off)[:, None], (T, LANES)).reshape(n, own, LANES)
        hbm = pl.BlockSpec(memory_space=pl.ANY)
        vm = pltpu.VMEM
        dma = pltpu.SemaphoreType.DMA
        g, dxf, dw1, loss = pl.pallas_call(
            functools.partial(_main, n, nb, T),
            out_shape=(jax.ShapeDtypeStruct((n, own, Vl), BF16),
                       jax.ShapeDtypeStruct((n, own, H), BF16),
                       jax.ShapeDtypeStruct((NT * TD, Vl), BF16),
                       jax.ShapeDtypeStruct((1, BT), F32)),
            in_specs=[hbm, hbm, hbm],
            out_specs=(hbm, hbm, hbm, pl.BlockSpec(memory_space=pltpu.VMEM)),
            scratch_shapes=[
                vm((3, n, R, LANES), jnp.int32),
                vm((BT, LANES), F32), vm((BT, LANES), F32), vm((BT, LANES), F32),
                vm((BT, LANES), F32), vm((BT, LANES), F32),
                vm((2, 8, BT), F32), vm((2, n, 8, BT), F32),
                vm((3, n // 2, 2, R, TH), F32), vm((NSL, n // 2, R, TH), F32),
                vm((NSL, 2, R // 2, TH), F32), vm((NSL, 2, R, TH), F32),
                vm((4, R, TH), F32), vm((NSL, 2, R, TH), F32), vm((NSL, R, TH), F32),
                vm((NS, R, TH), BF16),
                dma((NS,)), dma((2,)), dma((3,)), dma, dma((2, n)), dma((2, n)),
                dma((3,)), dma((NSL,)), dma((4, 2)), dma((NSL, 2)), dma((NSL, 2)),
                dma((NSL, 2)), dma((NS,)),
                dma((8, nb)), dma((8, nb)), dma((2,)), dma((NS,)), dma((2,)),
            ],
            compiler_params=pltpu.CompilerParams(
                collective_id=0, has_side_effects=True, vmem_limit_bytes=67043328),
            cost_estimate=pl.CostEstimate(flops=5 * T * H * Vl,
                                          bytes_accessed=2 * (H * Vl + T * (H + Vl)),
                                          transcendentals=2 * T * Vl),
            name="head_main",
        )(X.reshape(n, own, H), W, lab)
        tv = Vl // NS
        dW, dX, L = pl.pallas_call(
            functools.partial(_rest, 1.0 / T),
            out_shape=(jax.ShapeDtypeStruct((H, Vl), BF16), jax.ShapeDtypeStruct((T, H), BF16),
                       jax.ShapeDtypeStruct((1,), F32)),
            in_specs=[hbm, hbm, hbm, hbm, pl.BlockSpec(memory_space=pltpu.VMEM)],
            out_specs=(hbm, hbm, pl.BlockSpec(memory_space=pltpu.SMEM)),
            scratch_shapes=[vm((2, T, TD), BF16), vm((T, Vl), BF16), vm((2, TD, tv), BF16),
                            vm((16, 128, H), BF16),
                            dma((2,)), dma((NS,)), dma((2,)), dma((16,)), dma((16,))],
            compiler_params=pltpu.CompilerParams(vmem_limit_bytes=56 * 1024 * 1024),
            cost_estimate=pl.CostEstimate(flops=T * H * Vl,
                                          bytes_accessed=2 * (H * Vl + T * (H + Vl)),
                                          transcendentals=0),
            name="head_rest",
        )(X, g.reshape(T, Vl), dw1, dxf.reshape(T, H), loss)
        return L, dW, dX

    return jax.shard_map(local, mesh=mesh,
                         in_specs=(P('dp', None), P(None, 'tp'), P('dp')),
                         out_specs=(P('dp'), P('dp', 'tp'), P('dp', None)),
                         check_vma=False)
```

time: 700 us -> 314 us (0.45)
  blocking collectives: 376 us -> 0 us
  Pallas kernels: 0 us -> 311 us
  matrix products: 236 us -> 0 us
  local copies, waits for them, and re-layouts: 44.1 us -> 1.31 us
  other arithmetic: 39.5 us -> 0.7 us
    psum x2 -> x0, blocking collectives: 362 us -> none  [the longest x1 339 us: local(): dX = lax.psum(dXp, 'tp').astype(jnp.bfloat16)]
    pallas_call x0 -> x2, Pallas kernels: none -> 311 us  [the longest x1 271 us: local(): pl.pallas_call(functools.partial(_main, n, nb, T), out_shape=(jax.ShapeDt...]
    dot_general x3 -> x0, matrix products: 236 us -> none  [the longest x1 78.8 us: local(): Z = jnp.dot(X, W, preferred_element_type=jnp.float32)]
    unnamed x3 -> x0, local copies, waits for them, and re-layouts: 44.1 us -> none
    convert_element_type x1 -> x0, other arithmetic: 22.3 us -> none  [local(): ((jnp.exp(Z - M[:, None]) / S[:, None] - hit.astype(jnp.float32)) / T).as...]
    reduce_sum x2 -> x0, other arithmetic: 15.8 us -> none  [the longest x1 15.2 us: local(): s = jnp.exp(Z - m[:, None]).sum(axis=1)]
    pmax x1 -> x0, blocking collectives: 14.1 us -> none  [local(): M = lax.pmax(m, 'tp')]
where the time goes in v2:
time: 314 us
  Pallas kernels  311 us (99%)
    pallas_call x1, Pallas kernels, local(): pl.pallas_call(functools.partial(_main, n, nb, T), out_shape=(jax.ShapeDt...  271 us
    pallas_call x1, Pallas kernels, local(): pl.pallas_call(functools.partial(_rest, 1.0 / T), out_shape=(jax.ShapeDty...  39.7 us

profile of v2, /device:TPU:81, one launch (start us, length us, event | category | flops | bytes accessed | tf_op | source)
XLA Modules:
  0.0 313.8 jit_solution(7724939112576301562)
XLA Ops:
  0.6 0.7 broadcast_subtract_fusion
  1.3 1.3 broadcast_in_dim.9.lab_hbm
  2.6 271.2 %head_main.1 = (bf16[8,256,4096]{2,1,0:T(8,128)(2,1)}, bf16[8,256,4096]{2,1,0:T(8,128)(2,1)}, bf16[3072,4096]{1,0:T(8,128)(2,1)}, f32[1,256]{1,0:T(1,128)}) custom-call(bf16[8,256,4096]{2,1,0:T(8,128)(2,1)} %bitcast.3, bf16[4096,4096]{1,0:T(8,128)(2,1)} %w_hbm.1, s32[8,256,128]{2,1,0:T(8,128)} %broadcast_in_dim.9.lab_hbm), custom_call_target="tpu_custom_call" | custom-call | flops 171798691840 | bytes 67108864 | tf_op jit(solution)/shard_map/head_main/pallas_call | solution.py:593
  273.9 39.7 %head_rest.1 = (bf16[4096,4096]{1,0:T(8,128)(2,1)}, bf16[2048,4096]{1,0:T(8,128)(2,1)}, f32[1]{0:T(128)}) custom-call(bf16[2048,4096]{1,0:T(8,128)(2,1)} %x_hbm.1, bf16[2048,4096]{1,0:T(8,128)(2,1)} %bitcast.4, bf16[3072,4096]{1,0:T(8,128)(2,1)} %get-tuple-element.11.dw1_hbm, bf16[2048,4096]{1,0:T(8,128)(2,1)} %bitcast.5, f32[1,256]{1,0:T(1,128)} %get-tuple-element.13.loss_ref), custom_call_target="tpu_custom_call" | custom-call | flops 34359738368 | bytes 67108864 | tf_op jit(solution)/shard_map/head_rest/pallas_call | solution.py:623
  (1 shorter events, 0.0 us)

commit v3 on v2

--- a/solution.py
+++ b/solution.py
@@ -16,13 +16,13 @@
 NSL = 8
 LANES = 128
 TD = 512
-NT = 6
-
-
-def _main(n, nb, T, x_hbm, w_hbm, lab_hbm, g_hbm, dxf_hbm, dw1_hbm, loss_ref,
-          lab_v, m_s, s_s, t_s, mrep, rrep,
+NT = 5
+
+
+def _main(n, nb, T, x_hbm, w_hbm, lab_ref, g_hbm, dxf_hbm, dw1_hbm, loss_ref,
+          lab_v, lab_t, m_s, mr_s, s_s, t_s, mrep, rrep,
           st_send, st_v, dxb, d2d, r1, r2, s1, s2, fin, o_v,
-          w_sem, x_sem, lab_sem, g_sem, st_ssem, st_rsem,
+          w_sem, x_sem, g_sem, st_ssem, st_rsem,
           d2d_ssem, d2d_rsem, s1_ssem, r1_rsem, s2_ssem, r2_rsem, o_sem,
           ag_ssem, ag_rsem, xt_sem, gt_sem, ot_sem):
     nch = n // 2
@@ -42,8 +42,10 @@
     def rows_of(b):
         return pl.ds(pl.multiple_of(b * R, R), R)
 
-    def lab_copy(b):
-        return pltpu.make_async_copy(lab_hbm.at[:, rows_of(b), :], lab_v.at[b % 3], lab_sem.at[b % 3])
+    def lab_build(b):
+        lt = lab_t[rows_of(b), :]
+        for q in range(n):
+            lab_v[b % 2, q] = jnp.broadcast_to(lt[:, q:q + 1], (R, LANES))
 
     def st_copy(b, d):
         dev = (me + d) % n
@@ -222,21 +224,27 @@
             z_v[:, cols] = jnp.dot(x_v[b % 2].reshape(BT, H), w_v[:, cols],
                                           preferred_element_type=F32)
 
-        def stat_tile(b, j):
+        def z_cols(j, rows):
+            return [z_v[rows, pl.ds(pl.multiple_of(j * TN + k * LANES, LANES), LANES)]
+                    for k in range(TN // LANES)]
+
+        def stat_max(j):
             for r in range(0, BT, 16):
                 rows = pl.ds(r, 16)
-                lab = lab_v[b % 3].reshape(BT, LANES)[r:r + 16]
+                m_s[rows] = functools.reduce(jnp.maximum, z_cols(j, rows), m_s[rows])
+
+        def stat_sum(b, j):
+            for r in range(0, BT, 16):
+                rows = pl.ds(r, 16)
+                lab = lab_v[b % 2].reshape(BT, LANES)[r:r + 16]
                 ln = lane[r:r + 16]
-                zs = [z_v[rows, pl.ds(pl.multiple_of(j * TN + k * LANES, LANES), LANES)]
-                      for k in range(TN // LANES)]
-                m_old = m_s[rows]
-                m_new = functools.reduce(jnp.maximum, zs, m_old)
-                acc = s_s[rows] * jnp.exp(m_old - m_new)
+                m = m_s[rows]
+                acc = s_s[rows] * jnp.exp(mr_s[rows] - m)
                 tgt = t_s[rows]
-                for k, zk in enumerate(zs):
-                    acc = acc + jnp.exp(zk - m_new)
+                for k, zk in enumerate(z_cols(j, rows)):
+                    acc = acc + jnp.exp(zk - m)
                     tgt = tgt + jnp.where(lab == ln + (j * TN + k * LANES), zk, 0.0)
-                m_s[rows] = m_new
+                mr_s[rows] = m
                 s_s[rows] = acc
                 t_s[rows] = tgt
 
@@ -244,7 +252,7 @@
             rb = 2 * R
             for r in range(0, BT, rb):
                 rows = pl.ds(r, rb)
-                lab = lab_v[b % 3].reshape(BT, LANES)[r:r + rb]
+                lab = lab_v[b % 2].reshape(BT, LANES)[r:r + rb]
                 ln = lane[r:r + rb]
                 mm, rr = mrep[rows], rrep[rows]
                 for k in range(TN // LANES):
@@ -257,10 +265,11 @@
 
         def stats_init():
             m_s[...] = jnp.full((BT, LANES), -jnp.inf, F32)
+            mr_s[...] = jnp.full((BT, LANES), -jnp.inf, F32)
             s_s[...] = jnp.zeros((BT, LANES), F32)
             t_s[...] = jnp.zeros((BT, LANES), F32)
 
-        def stats_send(b):
+        def stats_final(b):
             ml = m_s[...]
             m = jnp.max(ml, axis=1, keepdims=True)
             s = jnp.sum(s_s[...] * jnp.exp(ml - m), axis=1, keepdims=True)
@@ -269,6 +278,8 @@
             a = a.T[0:8]
             st_send[b % 2] = a
             st_v[b % 2, me] = a
+
+        def stats_start(b):
             for d in range(1, n):
                 st_copy(b, d).start()
 
@@ -286,12 +297,13 @@
             mrep[...] = jnp.broadcast_to(a[:, 0:1], (BT, LANES))
             rrep[...] = jnp.broadcast_to(a[:, 1:2], (BT, LANES))
 
+        def d_free(u):
+            @pl.when(u >= 3)
+            def _():
+                d2d_copy(u - 3).wait_send()
+
         def d_tile(b, s):
             u = b * NS + s
-
-            @pl.when(u >= 3)
-            def _():
-                d2d_copy(u - 3).wait_send()
             gs = g_v[...].reshape(BT, Vl)
             dx = lax.dot_general(gs, w_v[pl.ds(pl.multiple_of(s * TH, TH), TH), :],
                                  (((1,), (1,)), ((), ())), preferred_element_type=F32)
@@ -302,30 +314,29 @@
             w_copy(j).start()
             if j == 0:
                 x_copy(0).start()
-                lab_copy(0).start()
-                lab_copy(1).start()
                 x_copy(1).start()
         loss_ref[...] = jnp.zeros_like(loss_ref)
         stats_init()
         x_copy(0).wait()
-        lab_copy(0).wait()
+        lab_t[...] = jnp.concatenate([lab_ref[...] - me * Vl] * (LANES // n), axis=0).T
+        lab_build(0)
 
         @pl.loop(0, NS)
         def _(j):
             w_copy(j).wait()
             z_tile(0, j)
 
-        @pl.loop(0, NS)
-        def _(j):
-            stat_tile(0, j)
-        stats_send(0)
+            @pl.loop(0, 1)
+            def _(_):
+                stat_max(j)
+                stat_sum(0, j)
+        stats_final(0)
+        stats_start(0)
 
         @pl.loop(1, nb)
         def _(i):
             x_copy(i).wait()
-            lab_copy(i).wait()
-            stats_recv(i - 1)
-            stats_init()
+            lab_build(i)
 
             @pl.when(i >= 2)
             def _():
@@ -334,25 +345,45 @@
             @pl.when(i + 1 < nb)
             def _():
                 x_copy(i + 1).start()
-                lab_copy(i + 1).start()
 
             @pl.loop(0, NS)
             def _(j):
+                @pl.when(j >= 2)
+                def _():
+                    stat_sum(i, j - 2)
                 comm_z(i, j)
 
-                @pl.when(j > 0)
+                @pl.when(j == 0)
                 def _():
-                    stat_tile(i, j - 1)
-                g_tile(i - 1, j)
-                z_tile(i, j)
-            stat_tile(i, NS - 1)
-            stats_send(i)
+                    stats_recv(i - 1)
+                    stats_init()
+                    g_tile(i - 1, 0)
+                    z_tile(i, 0)
+
+                @pl.when(j >= 1)
+                def _():
+                    stat_max(j - 1)
+                    g_tile(i - 1, j)
+                    z_tile(i, j)
             g_copy(i - 1).start()
 
             @pl.loop(0, NS)
             def _(s):
                 comm_d(i, s)
-                d_tile(i - 1, s)
+                d_free((i - 1) * NS + s)
+
+                @pl.when(s == 0)
+                def _():
+                    stat_max(NS - 1)
+                    stat_sum(i, NS - 2)
+                    stat_sum(i, NS - 1)
+                    stats_final(i)
+                    d_tile(i - 1, 0)
+                    stats_start(i)
+
+                @pl.when(s > 0)
+                def _():
+                    d_tile(i - 1, s)
 
         stats_recv(nb - 1)
         g_copy(nb - 2).wait()
@@ -366,6 +397,7 @@
         @pl.loop(0, NS)
         def _(s):
             comm_d(nb, s)
+            d_free((nb - 1) * NS + s)
             d_tile(nb - 1, s)
 
         g_copy(nb - 1).wait()
@@ -417,7 +449,7 @@
                                        (6, (ag_a, 4)), (6, (ag_a, 5)), (9, (ag_a, 6)),
                                        (12, (o_wait, 7)), (12, (ag_a, 7)), (13, (ag_c, 3)),
                                        (14, (ag_b, 4)), (17, (ag_b, 5)), (19, (ag_b, 6)),
-                                       (22, (ag_c, 4)), (22, (ag_b, 7)), (23, (ag_c, 5))):
+                                       (19, (ag_c, 4)), (19, (ag_b, 7)), (19, (ag_c, 5))):
                 @pl.when(t == when_)
                 def _(step_=step_, k0=k0):
                     step_(k0)
@@ -524,29 +556,16 @@
         pltpu.make_async_copy(cb.at[c % nbuf], dx_hbm.at[pl.ds(0, rows)], wr_sem.at[c % nbuf]).wait()
 
     xt_copy(0).start()
-    for v in range(nv):
+    gt_copy(0).start()
+    for v in range(1, nv):
         gt_copy(v).start()
-    for c in range(ahead):
-        rd_start(c)
+        for c in range(ahead * (v - 1) // (nv - 1), ahead * v // (nv - 1)):
+            rd_start(c)
     l_ref[0] = jnp.sum(loss_ref[...]) * inv_t
 
     @pl.loop(0, nh * nv)
     def _(t):
         h, v = t // nv, t % nv
-
-        @pl.loop(0, per)
-        def _(q):
-            c = t * per + q
-
-            @pl.when(c < nc)
-            def _():
-                rd_wait(c)
-                wr_start(c)
-
-                @pl.when(c >= ahead)
-                def _():
-                    wr_wait(c - ahead)
-                rd_start(c + ahead)
 
         @pl.when(v == 0)
         def _():
@@ -567,6 +586,20 @@
         ot[t % 2] = lax.dot_general(xt[h % 2], gt[:, cols], (((0,), (0,)), ((), ())),
                                     preferred_element_type=F32).astype(BF16)
         ot_copy(t).start()
+
+        @pl.loop(0, per)
+        def _(q):
+            c = t * per + q
+
+            @pl.when(c < nc)
+            def _():
+                rd_wait(c)
+                wr_start(c)
+
+                @pl.when(c >= ahead)
+                def _():
+                    wr_wait(c - ahead)
+                rd_start(c + ahead)
 
     for t in range(nh * nv - 2, nh * nv):
         ot_copy(t).wait()
@@ -585,8 +618,7 @@
         nb = own // R
         BT = n * R
         TH = H // NS
-        off = lax.axis_index("tp") * Vl
-        lab = jnp.broadcast_to((labels - off)[:, None], (T, LANES)).reshape(n, own, LANES)
+        lab = labels.reshape(n, own)
         hbm = pl.BlockSpec(memory_space=pl.ANY)
         vm = pltpu.VMEM
         dma = pltpu.SemaphoreType.DMA
@@ -596,18 +628,18 @@
                        jax.ShapeDtypeStruct((n, own, H), BF16),
                        jax.ShapeDtypeStruct((NT * TD, Vl), BF16),
                        jax.ShapeDtypeStruct((1, BT), F32)),
-            in_specs=[hbm, hbm, hbm],
+            in_specs=[hbm, hbm, pl.BlockSpec(memory_space=pltpu.VMEM)],
             out_specs=(hbm, hbm, hbm, pl.BlockSpec(memory_space=pltpu.VMEM)),
             scratch_shapes=[
-                vm((3, n, R, LANES), jnp.int32),
+                vm((2, n, R, LANES), jnp.int32), vm((own, LANES), jnp.int32),
                 vm((BT, LANES), F32), vm((BT, LANES), F32), vm((BT, LANES), F32),
-                vm((BT, LANES), F32), vm((BT, LANES), F32),
+                vm((BT, LANES), F32), vm((BT, LANES), F32), vm((BT, LANES), F32),
                 vm((2, 8, BT), F32), vm((2, n, 8, BT), F32),
                 vm((3, n // 2, 2, R, TH), F32), vm((NSL, n // 2, R, TH), F32),
                 vm((NSL, 2, R // 2, TH), F32), vm((NSL, 2, R, TH), F32),
                 vm((4, R, TH), F32), vm((NSL, 2, R, TH), F32), vm((NSL, R, TH), F32),
                 vm((NS, R, TH), BF16),
-                dma((NS,)), dma((2,)), dma((3,)), dma, dma((2, n)), dma((2, n)),
+                dma((NS,)), dma((2,)), dma, dma((2, n)), dma((2, n)),
                 dma((3,)), dma((NSL,)), dma((4, 2)), dma((NSL, 2)), dma((NSL, 2)),
                 dma((NSL, 2)), dma((NS,)),
                 dma((8, nb)), dma((8, nb)), dma((2,)), dma((NS,)), dma((2,)),

time: 314 us -> 311 us (level)
  no operation moved by 1% of the time
where the time goes in v3:
time: 311 us
  Pallas kernels  309 us (99%)
    pallas_call x1, Pallas kernels, local(): pl.pallas_call(functools.partial(_main, n, nb, T), out_shape=(jax.ShapeDt...  269 us
    pallas_call x1, Pallas kernels, local(): pl.pallas_call(functools.partial(_rest, 1.0 / T), out_shape=(jax.ShapeDty...  40.5 us

profile of v3, /device:TPU:81, one launch (start us, length us, event | category | flops | bytes accessed | tf_op | source)
XLA Modules:
  0.0 311.1 jit_solution(12295403969578149713)
XLA Ops:
  0.6 1.3 reshape.19.lab_ref
  1.9 268.5 %head_main.1 = (bf16[8,256,4096]{2,1,0:T(8,128)(2,1)}, bf16[8,256,4096]{2,1,0:T(8,128)(2,1)}, bf16[2560,4096]{1,0:T(8,128)(2,1)}, f32[1,256]{1,0:T(1,128)}) custom-call(bf16[8,256,4096]{2,1,0:T(8,128)(2,1)} %bitcast.3, bf16[4096,4096]{1,0:T(8,128)(2,1)} %w_hbm.1, s32[8,256]{1,0:T(8,128)} %reshape.19.lab_ref), custom_call_target="tpu_custom_call" | custom-call | flops 171798691840 | bytes 67108864 | tf_op jit(solution)/shard_map/head_main/pallas_call | solution.py:625
  270.5 40.5 %head_rest.1 = (bf16[4096,4096]{1,0:T(8,128)(2,1)}, bf16[2048,4096]{1,0:T(8,128)(2,1)}, f32[1]{0:T(128)}) custom-call(bf16[2048,4096]{1,0:T(8,128)(2,1)} %x_hbm.1, bf16[2048,4096]{1,0:T(8,128)(2,1)} %bitcast.4, bf16[2560,4096]{1,0:T(8,128)(2,1)} %get-tuple-element.11.dw1_hbm, bf16[2048,4096]{1,0:T(8,128)(2,1)} %bitcast.5, f32[1,256]{1,0:T(1,128)} %get-tuple-element.13.loss_ref), custom_call_target="tpu_custom_call" | custom-call | flops 34359738368 | bytes 67108864 | tf_op jit(solution)/shard_map/head_rest/pallas_call | solution.py:655
